TPU v7x, 32 devices: a whole 2x2x4 slice. The times are simulated.
32 devices in a mesh: seq: 8 (over y, x, core), tp: 4 (over z).
Axes of the slice: x: 2, y: 2, z: 4, core: 2. Of those that a mesh axis runs over, the one named last changes fastest.
Arguments:
- hidden: bfloat16 [4096, 4096], P('seq', 'tp'), may hold values from -6 to 6
- norm_gain: float32 [4096], P('tp'), may hold values from 0.5 to 1.5
- rank_down: bfloat16 [4096, 1024], P('tp'), may hold values from -0.09375 to 0.09375
- gate_up: bfloat16 [1024, 4096], P(None, 'tp'), may hold values from -0.1875 to 0.1875
- value_up: bfloat16 [1024, 4096], P(None, 'tp'), may hold values from -0.1875 to 0.1875
- state_up: bfloat16 [1024, 1024], P(None, 'tp'), may hold values from -0.1875 to 0.1875
- step_up: bfloat16 [1024, 64], P(None, 'tp'), may hold values from -0.1875 to 0.1875
- conv_value: float32 [4, 4096], P(None, 'tp'), may hold values from -3 to 3
- conv_state: float32 [4, 1024], P(None, 'tp'), may hold values from -3 to 3
- step_bias: float32 [64], P('tp'), may hold values from -6.9 to -2.3
- decay_log: float32 [64], P('tp'), may hold values from -11 to 2.77
- skip_gain: float32 [64], P('tp'), may hold values from 0.5 to 1.5
- gate_gain: float32 [4096], P('tp'), may hold values from 0.5 to 1.5
- out_down: bfloat16 [4096, 1024], P('tp'), may hold values from -0.09375 to 0.09375
- out_up: bfloat16 [1024, 4096], P(None, 'tp'), may hold values from -0.1875 to 0.1875
Outputs:
- block_out: bfloat16 [4096, 4096], P('seq', 'tp')
All inputs are finite; a program needn't handle non-finite values.
Results may differ from a plain program's by a relative error of at most 0.012.
Values may be sent and summed in bfloat16 or wider, within the bound.
A program may use at most 64 MiB of HBM per device.

v0:
```python
import jax
import jax.numpy as jnp
from jax import lax
from jax.sharding import PartitionSpec as P

HEAD_DIM = 64
NSTATE = 128
GROUPS = 4
epsilon = 1e-05
highest = lax.Precision.HIGHEST


def shifted(shard, axis, by):
    peers = lax.axis_size(axis)
    pairs = [(i, i + by) for i in range(peers) if 0 <= i + by < peers]
    return lax.ppermute(shard, axis, pairs)


def entering(part, axis, combine, identity):
    place = lax.axis_index(axis)
    gathered = jax.tree.map(lambda a: lax.all_gather(a, axis), part)
    state = jax.tree.map(lambda a, e: jnp.zeros_like(a) + jnp.asarray(e, a.dtype), part, identity)

    def one(lap, state):
        return combine(
            state, jax.tree.map(lambda a: lax.dynamic_index_in_dim(a, lap, 0, False), gathered)
        )

    return lax.fori_loop(0, place, one, state)


def contract_rows(left, right):
    return lax.dot_general(
        left, right, (((0,), (0,)), ((), ())), preferred_element_type=jnp.float32
    )


def contract_columns(columns, rows):
    return lax.dot_general(
        columns, rows, (((0,), (1,)), ((), ())), preferred_element_type=jnp.float32
    )


def depthwise(rim_rows, current, weights):
    joined = jnp.concatenate([rim_rows, current], axis=0).astype(jnp.float32)
    length = current.shape[0]
    result = jnp.zeros(current.shape, jnp.float32)
    for offset in range(weights.shape[0]):
        result = result + weights[offset] * joined[offset : offset + length]
    return jax.nn.silu(result).astype(jnp.bfloat16)


def on_device(
    hidden,
    norm_gain,
    rank_down,
    gate_up,
    value_up,
    state_up,
    step_up,
    conv_value,
    conv_state,
    step_bias,
    decay_log,
    skip_gain,
    gate_gain,
    out_down,
    out_up,
):
    tokens = hidden.shape[0]
    tp_count = lax.axis_size("tp")
    tp_index = lax.axis_index("tp")
    model_width = hidden.shape[1] * tp_count
    hidden_wide = hidden.astype(jnp.float32)
    local_squares = jnp.sum(hidden_wide * hidden_wide, axis=1)
    scaled = (hidden_wide * norm_gain).astype(jnp.bfloat16)
    up_weights = (gate_up, value_up, state_up, step_up)
    partial_value = jnp.dot(scaled, rank_down, preferred_element_type=jnp.float32)
    summed, total_squares = lax.psum((partial_value, local_squares), "tp")
    factor = lax.rsqrt(total_squares / model_width + epsilon)
    reduced = (summed * factor[:, None]).astype(jnp.bfloat16)
    projected = tuple(
        (jnp.dot(reduced, weight, preferred_element_type=jnp.float32) for weight in up_weights)
    )
    gate_pre = projected[0].astype(jnp.bfloat16)
    value_pre = projected[1].astype(jnp.bfloat16)
    state_pre = projected[2].astype(jnp.bfloat16)
    step_pre = projected[3].astype(jnp.bfloat16)
    rim_start = tokens - conv_value.shape[0] + 1
    rim_value, rim_state = shifted((value_pre[rim_start:], state_pre[rim_start:]), "seq", 1)
    value_act = depthwise(rim_value, value_pre, conv_value)
    state_act = depthwise(rim_state, state_pre, conv_state)
    state_all = lax.all_gather(state_act, "tp", axis=1, tiled=True)
    heads_local = decay_log.shape[0]
    heads_total = heads_local * tp_count
    group_index = tp_index * heads_local // (heads_total // GROUPS)
    inward = lax.dynamic_slice_in_dim(state_all, group_index * NSTATE, NSTATE, 1).astype(
        jnp.float32
    )
    outward = lax.dynamic_slice_in_dim(
        state_all, (GROUPS + group_index) * NSTATE, NSTATE, 1
    ).astype(jnp.float32)
    step_size = jax.nn.softplus(step_pre.astype(jnp.float32) + step_bias)
    log_decay = jnp.cumsum(-jnp.exp(decay_log) * step_size, axis=0)
    values = value_act.astype(jnp.float32).reshape(tokens, heads_local, HEAD_DIM)
    coupling = jnp.dot(outward, inward.T, precision=highest)
    positions = jnp.arange(tokens)
    causal = positions[:, None] >= positions[None, :]
    spread = log_decay.T[:, :, None] - log_decay.T[:, None, :]
    attenuation = jnp.where(causal[None], jnp.exp(jnp.where(causal[None], spread, 0.0)), 0.0)
    mixing = coupling[None] * attenuation * step_size.T[:, None, :]
    within = jnp.einsum("hts,shp->thp", mixing, values, precision=highest)
    ending = jnp.exp(log_decay[-1][None, :] - log_decay) * step_size
    local_state = jnp.einsum("sh,shp,sn->hpn", ending, values, inward, precision=highest)
    local_decay = jnp.exp(log_decay[-1])

    def combine(earlier, later):
        return (earlier[0] * later[0], later[0][:, None, None] * earlier[1] + later[1])

    prefix = entering(
        (local_decay, local_state),
        "seq",
        combine,
        (jnp.ones_like(local_decay), jnp.zeros_like(local_state)),
    )
    incoming = prefix[1]
    carried_in = jnp.exp(log_decay)[:, :, None] * jnp.einsum(
        "tn,hpn->thp", outward, incoming, precision=highest
    )
    mixed = (within + carried_in + skip_gain[None, :, None] * values).reshape(
        tokens, heads_local * HEAD_DIM
    )
    gated = mixed * jax.nn.silu(gate_pre.astype(jnp.float32))
    group_width = heads_total * HEAD_DIM // GROUPS
    selector = (jnp.arange(GROUPS) == group_index).astype(jnp.float32)
    group_sums = lax.psum(jnp.sum(gated * gated, axis=1)[:, None] * selector[None, :], "tp")
    own_sum = jnp.sum(group_sums * selector[None, :], axis=1)
    normed = (gated * lax.rsqrt(own_sum / group_width + epsilon)[:, None] * gate_gain).astype(
        jnp.bfloat16
    )
    out_share = lax.psum_scatter(
        contract_columns(out_down, normed), "tp", scatter_dimension=0, tiled=True
    ).astype(jnp.bfloat16)
    update = contract_rows(lax.all_gather(out_share, "tp", axis=0, tiled=True), out_up)
    return (hidden_wide + update).astype(jnp.bfloat16)


def solution(mesh):
    return jax.shard_map(
        on_device,
        mesh=mesh,
        in_specs=(
            P("seq", "tp"),
            P("tp"),
            P("tp", None),
            P(None, "tp"),
            P(None, "tp"),
            P(None, "tp"),
            P(None, "tp"),
            P(None, "tp"),
            P(None, "tp"),
            P("tp"),
            P("tp"),
            P("tp"),
            P("tp"),
            P("tp", None),
            P(None, "tp"),
        ),
        out_specs=P("seq", "tp"),
        check_vma=False,
    )
```

profile of v0, /device:TPU:0, one launch (start us, length us, event | category | flops | bytes accessed | tf_op | source)
XLA Modules:
  0.0 310.0 jit_solution(9953234598632457863)
XLA Ops:
  6.5 0.0 copy-start
  6.5 0.0 all-reduce.2.cloned.1.call-start
  6.5 4.6 %fusion.29 = f32[512,1024]{1,0:T(8,128)} fusion(bf16[1024,1024]{1,0:T(8,128)(2,1)} %param.19, bf16[512,1024]{1,0:T(8,128)(2,1)} %param.17, f32[1024]{0:T(1024)} %param.18), kind=kOutput, calls=%fused_computation.51 | convolution fusion | flops 1075314688 | bytes 5246976 | tf_op jit(solution)/shard_map/dot_general | solution.py:78
  11.2 0.0 all-reduce.2.cloned.1.call-update
  11.2 0.0 all-gather.6.cloned.1.call-start
  11.3 1.1 copy-done.4
  12.4 0.3 fusion.20
  12.7 13.9 %psum.22 = f32[512]{0:T(512)S(1)} all-reduce(f32[512]{0:T(512)S(1)} %fusion.20), channel_id=1, replica_groups=mesh['seq'=8,'tp'=4] {'tp'}, use_global_device_ids=true, to_apply=%region_2.0 | all-reduce | flops 512 | bytes 4096 | tf_op jit(solution)/shard_map/psum | solution.py:79
  26.5 0.0 copy-done.13
  26.6 0.0 copy-done.9
  26.6 0.6 fusion.57
  27.2 0.0 copy-done.8
  27.2 73.1 %all-reduce.2.cloned.1.call-done = f32[512,1024]{1,0:T(8,128)} async-done(((f32[512,1024]{1,0:T(8,128)}), f32[512,1024]{1,0:T(8,128)}) %all-reduce.2.cloned.1.call-update) | async-done | bytes 2097168 | tf_op jit(solution)/shard_map/psum | solution.py:79
  100.3 1.8 multiply_convert_fusion.2
  102.2 0.0 copy-done.7
  102.2 0.4 fusion.28
  102.6 0.1 compare_select_fusion.1
  102.7 0.4 convolution_convert_fusion.2
  103.1 0.6 slice.90
  103.7 2.0 collective-permute-start.1
  105.7 1.1 reduce-window.6
  106.8 0.2 slice_reduce_fusion
  107.0 0.0 collective-permute-done.1
  107.0 0.7 maximum_convert_fusion.1
  107.7 1.7 multiply_convert_fusion.4
  109.4 0.0 all-gather.6.cloned.1.call-update
  109.5 0.0 all-gather.10.cloned.1.call-start
  109.5 0.0 copy-done.2
  109.5 2.8 convolution_convert_fusion.1
  112.4 3.4 %collective-permute-start = (bf16[3,1024]{1,0:T(4,128)(2,1)S(1)}, bf16[3,1024]{1,0:T(4,128)(2,1)S(1)}, u32[]{:S(2)}, u32[]{:S(2)}) collective-permute-start(bf16[3,1024]{1,0:T(4,128)(2,1)S(1)} %slice.85), channel_id=1, source_target_pairs={{0,4},{4,8},{8,12},{12,16},{16,20},{20,24},{24,28},{1,5},{5,9},{9,... | collective-permute-start | bytes 18440 | tf_op jit(solution)/shard_map/ppermute | solution.py:16
  115.8 0.1 copy_bitcast_fusion
  115.9 0.2 slice_reduce_fusion.1
  116.1 0.1 bitcast_exponential_fusion
  116.2 0.4 collective-permute-done
  116.7 0.3 maximum_convert_fusion
  117.0 1.3 multiply_convert_fusion.1
  118.2 1.3 copy.29
  119.6 21.0 %all-gather.6.cloned.1.call-done = bf16[512,1024]{1,0:T(8,128)(2,1)} async-done(((bf16[512,256]{1,0:T(8,128)(2,1)}), bf16[512,1024]{1,0:T(8,128)(2,1)}) %all-gather.6.cloned.1.call-update) | async-done | bytes 1048592 | tf_op jit(solution)/shard_map/all_gather | solution.py:93
  140.6 3.2 %fusion.13 = f32[16,64,128]{2,1,0:T(8,128)} fusion(bf16[512,16,64]{0,2,1:T(8,128)(2,1)} %bitcast.86, f32[512,16]{0,1:T(8,128)S(1)} %get-tuple-element.63, bf16[512,1024]{1,0:T(8,128)(2,1)} %all-gather.6.cloned.1.call-done, s32[]{:T(128)S(6)} %select_n.35), kind=kOutput, calls=%fused_computation.22 | convolution fusion | flops 806354944 | bytes 1736708 | tf_op jit(solution)/shard_map/sh,shp,sn->hpn/dot_general | solution.py:114
  143.8 0.0 all-gather.10.cloned.1.call-update
  143.8 0.0 reduce-scatter.2.cloned.1.call-start
  143.9 0.1 iota_compare_fusion
  143.9 7.9 %all-gather.1 = f32[8,1,16]{2,1,0:T(1,128)S(1)} all-gather(f32[1,1,16]{2,1,0:T(1,128)S(1)} %bitcast.100), channel_id=1, replica_groups=mesh['seq'=8,'tp'=4] {'seq'}, dimensions={0}, use_global_device_ids=true | all-gather | bytes 576 | tf_op jit(solution)/shard_map/all_gather | solution.py:21
  151.9 2.3 fusion.42
  154.1 24.7 %all-gather.10.cloned.1.call-done = f32[128,64,128]{2,1,0:T(8,128)} async-done(((f32[16,64,128]{2,1,0:T(8,128)}), f32[128,64,128]{2,1,0:T(8,128)}) %all-gather.10.cloned.1.call-update) | async-done | bytes 4194320 | tf_op jit(solution)/shard_map/all_gather | solution.py:21
  178.9 0.2 while.12
  179.1 0.0 copy-start.1
  179.1 0.0 copy-start.14
  179.1 2.0 fusion.39
  181.2 14.3 %fusion.14 = f32[512,16,64]{0,2,1:T(8,128)} fusion(bf16[512,16,64]{0,2,1:T(8,128)(2,1)S(1)} %bitcast.87, f32[512,16,64]{0,2,1:T(8,128)S(1)} %fusion.39, f32[16,512]{1,0:T(8,128)S(1)} %get-tuple-element.66, f32[16,512]{1,0:T(8,128)S(1)} %get-tuple-element.64, f32[512,512]{1,0:T(8,128)S(1)} %copy-done.6, pred[512,512]{1,0:T(8,128)(4,1)S(1)} %iota_compare_fusion, ...), kind=kOutput, calls=%fused_computation.23 | convolution fusion | flops 3244818432 | bytes 6651968 | tf_op jit(solution)/shard_map/hts,shp->thp/dot_general | solution.py:112
  195.5 3.0 copy.32
  198.5 4.5 %multiply_reduce_fusion = (f32[512]{0:T(512)S(1)}, f32[512,1024]{1,0:T(8,128)}) fusion(f32[512,1024]{1,0:T(8,128)} %copy.32, bf16[512,1024]{1,0:T(8,128)(2,1)S(1)} %copy-done.3, bf16[1024,1024]{1,0:T(8,128)(2,1)S(1)} %copy-done), kind=kOutput, calls=%fused_computation.40 | convolution fusion | flops 1078459904 | bytes 7342080 | tf_op jit(solution)/shard_map/dot_general | solution.py:83
  203.0 0.1 broadcast_multiply_fusion
  203.1 11.8 %psum.23 = f32[512,4]{0,1:T(4,128)S(1)} all-reduce(f32[512,4]{0,1:T(4,128)S(1)} %broadcast_multiply_fusion), channel_id=1, replica_groups=mesh['seq'=8,'tp'=4] {'tp'}, use_global_device_ids=true, to_apply=%region_8.9 | all-reduce | flops 2048 | bytes 16384 | tf_op jit(solution)/shard_map/psum | solution.py:136
  214.9 0.1 multiply_reduce_fusion.1
  215.0 4.8 %convolution_bitcast_fusion = f32[1024,512]{0,1:T(8,128)} fusion(bf16[1024,1024]{1,0:T(8,128)(2,1)} %param.30, f32[512,1024]{1,0:T(8,128)} %get-tuple-element.77, f32[1024]{0:T(1024)S(1)} %copy-done.12, f32[512]{0:T(512)S(1)} %add_rsqrt_fusion), kind=kOutput, calls=%fused_computation.43 | convolution fusion | flops 1075314688 | bytes 6297600 | tf_op jit(solution)/shard_map/dot_general | solution.py:39
  219.8 0.0 reduce-scatter.2.cloned.1.call-update
  219.9 0.0 all-gather.8.cloned.1.call-start
  219.9 48.4 %reduce-scatter.2.cloned.1.call-done = f32[256,512]{0,1:T(8,128)} async-done(((f32[1024,512]{0,1:T(8,128)}), f32[256,512]{0,1:T(8,128)}) %reduce-scatter.2.cloned.1.call-update) | async-done | bytes 524304 | tf_op jit(solution)/shard_map/reduce_scatter | solution.py:141
  268.3 1.8 convert_element_type.79
  270.1 0.0 all-gather.8.cloned.1.call-update
  270.1 29.3 %all-gather.8.cloned.1.call-done = bf16[1024,512]{0,1:T(8,128)(2,1)} async-done(((bf16[256,512]{0,1:T(8,128)(2,1)}), bf16[1024,512]{0,1:T(8,128)(2,1)}) %all-gather.8.cloned.1.call-update) | async-done | bytes 1048592 | tf_op jit(solution)/shard_map/all_gather | solution.py:144
  299.4 0.0 copy-done.5
  299.4 4.1 %fusion.21 = bf16[512,1024]{1,0:T(8,128)(2,1)} fusion(bf16[512,1024]{1,0:T(8,128)(2,1)S(1)} %copy-done.5, bf16[1024,512]{0,1:T(8,128)(2,1)} %all-gather.8.cloned.1.call-done, bf16[1024,1024]{1,0:T(8,128)(2,1)} %param.31), kind=kOutput, calls=%fused_computation.30 | convolution fusion | flops 1075314688 | bytes 5242880 | tf_op jit(solution)/shard_map/dot_general | solution.py:33
  (30 shorter events, 0.2 us)
Async XLA Ops:
  6.5 192.0 %copy-start = (bf16[1024,1024]{1,0:T(8,128)(2,1)S(1)}, bf16[1024,1024]{1,0:T(8,128)(2,1)}, u32[]{:S(2)}) copy-start(bf16[1024,1024]{1,0:T(8,128)(2,1)} %param.20) | copy-start | bytes 6291460
  6.5 93.8 %all-reduce.2.cloned.1.call-start = ((), (), s32[]{:S(2)}) async-start(), calls=%async_computation.1 | async-start | bytes 4194304 | tf_op jit(solution)/shard_map/psum | solution.py:79
  11.2 1.2 copy-start.4
  11.2 15.4 %copy-start.13 = (f32[16]{0:T(128)S(1)}, f32[16]{0:T(128)}, u32[]{:S(2)}) copy-start(f32[16]{0:T(128)} %param.27) | copy-start | bytes 196
  11.2 15.4 %copy-start.9 = (f32[4,256]{1,0:T(4,128)S(1)}, f32[4,256]{1,0:T(4,128)}, u32[]{:S(2)}) copy-start(f32[4,256]{1,0:T(4,128)} %param.25) | copy-start | bytes 12292
  11.2 16.0 %copy-start.8 = (f32[4,1024]{1,0:T(4,128)S(1)}, f32[4,1024]{1,0:T(4,128)}, u32[]{:S(2)}) copy-start(f32[4,1024]{1,0:T(4,128)} %param.24) | copy-start | bytes 49156
  11.2 129.4 %all-gather.6.cloned.1.call-start = ((), (), s32[]{:S(2)}) async-start(), calls=%async_computation.2 | async-start | bytes 1310720 | tf_op jit(solution)/shard_map/all_gather | solution.py:93
  12.4 89.8 %copy-start.7 = (bf16[1024,16]{0,1:T(8,128)(2,1)S(1)}, bf16[1024,16]{0,1:T(8,128)(2,1)}, u32[]{:S(2)}) copy-start(bf16[1024,16]{0,1:T(8,128)(2,1)} %param.23) | copy-start | bytes 98308
  12.4 89.8 %copy-start.10 = (f32[16]{0:T(128)S(1)}, f32[16]{0:T(128)}, u32[]{:S(2)}) copy-start(f32[16]{0:T(128)} %param.26) | copy-start | bytes 196
  100.3 2.3 copy-start.11
  102.2 7.3 %copy-start.2 = (bf16[512,1024]{1,0:T(8,128)(2,1)}, bf16[512,1024]{1,0:T(8,128)(2,1)S(1)}, u32[]{:S(2)}) copy-start(bf16[512,1024]{1,0:T(8,128)(2,1)S(1)} %multiply_convert_fusion.2) | copy-start | bytes 3145732
  103.7 3.3 %collective-permute-start.1 = (bf16[3,256]{1,0:T(4,128)(2,1)}, bf16[3,256]{1,0:T(4,128)(2,1)}, u32[]{:S(2)}, u32[]{:S(2)}) collective-permute-start(bf16[3,256]{1,0:T(4,128)(2,1)} %slice.90), channel_id=1, source_target_pairs={{0,4},{4,8},{8,12},{12,16},{16,20},{20,24},{24,28},{1,5},{5,9},{9,... | collective-permute-start | bytes 4616 | tf_op jit(solution)/shard_map/ppermute | solution.py:16
  109.5 69.4 %all-gather.10.cloned.1.call-start = ((), (), s32[]{:S(2)}) async-start(), calls=%async_computation.5 | async-start | bytes 4718592 | tf_op jit(solution)/shard_map/all_gather | solution.py:21
  112.4 4.3 %collective-permute-start = (bf16[3,1024]{1,0:T(4,128)(2,1)S(1)}, bf16[3,1024]{1,0:T(4,128)(2,1)S(1)}, u32[]{:S(2)}, u32[]{:S(2)}) collective-permute-start(bf16[3,1024]{1,0:T(4,128)(2,1)S(1)} %slice.85), channel_id=1, source_target_pairs={{0,4},{4,8},{8,12},{12,16},{16,20},{20,24},{24,28},{1,5},{5,9},{9,... | collective-permute-start | bytes 18440 | tf_op jit(solution)/shard_map/ppermute | solution.py:16
  143.8 124.5 %reduce-scatter.2.cloned.1.call-start = ((), (), s32[]{:S(2)}) async-start(), calls=%async_computation.3 | async-start | bytes 2621440 | tf_op jit(solution)/shard_map/reduce_scatter | solution.py:141
  179.1 2.1 copy-start.1
  179.1 2.1 copy-start.6
  179.1 2.1 copy-start.14
  195.5 3.0 copy-start.3
  198.5 16.5 %copy-start.12 = (f32[1024]{0:T(1024)S(1)}, f32[1024]{0:T(1024)}, u32[]{:S(2)}) copy-start(f32[1024]{0:T(1024)} %param.29) | copy-start | bytes 12292
  219.8 79.5 %copy-start.5 = (bf16[512,1024]{1,0:T(8,128)(2,1)S(1)}, bf16[512,1024]{1,0:T(8,128)(2,1)}, u32[]{:S(2)}) copy-start(bf16[512,1024]{1,0:T(8,128)(2,1)} %param.17) | copy-start | bytes 3145732
  219.9 79.5 %all-gather.8.cloned.1.call-start = ((), (), s32[]{:S(2)}) async-start(), calls=%async_computation.4 | async-start | bytes 1310720 | tf_op jit(solution)/shard_map/all_gather | solution.py:144
Sparse Core Ops, SparseCore 0:
  11.3 88.9 all-reduce.1
  109.6 30.9 all-gather.5
  143.9 34.8 all-gather.9
  220.0 48.2 reduce-scatter.1
  270.2 29.1 all-gather.7
where the time goes:
time: 311 us; the launch traced here: 310 us
  waiting for transfers between devices  197 us (63%)
  matrix products  43.6 us (14%)
  blocking collectives  33.6 us (11%)
  between operations  13.4 us (4%)
  other arithmetic  9.56 us (3%)
  local copies, waits for them, and re-layouts  7.12 us (2%)
  starting transfers between devices  5.58 us (2%)
    psum x1, waiting for transfers between devices, on_device(): summed, total_squares = lax.psum((partial_value, local_squares), 'tp')  73.1 us
    reduce_scatter x1, waiting for transfers between devices, on_device(): lax.psum_scatter(contract_columns(out_down, normed), 'tp', scatter_dimens...  48.4 us
    all_gather x1, waiting for transfers between devices, on_device(): lax.all_gather(out_share, 'tp', axis=0, tiled=True)  29.3 us
    all_gather x1, waiting for transfers between devices, entering(): gathered = jax.tree.map(lambda a: lax.all_gather(a, axis), part)  24.7 us
    all_gather x1, waiting for transfers between devices, on_device(): state_all = lax.all_gather(state_act, 'tp', axis=1, tiled=True)  21 us
    dot_general x1, matrix products, on_device(): within = jnp.einsum('hts,shp->thp', mixing, values, precision=highest)  14.3 us
    psum x1, blocking collectives, on_device(): summed, total_squares = lax.psum((partial_value, local_squares), 'tp')  13.9 us
    psum x1, blocking collectives, on_device(): lax.psum(jnp.sum(gated * gated, axis=1)[:, None] * selector[None, :], 'tp')  11.8 us
  transfers between devices with their start and end apart: 7, of which 6 were waited for; matrix products, arithmetic and copies ran while one was open for 3% of the time, Pallas kernels for 0%

commit v1 on v0

--- a/solution.py
+++ b/solution.py
@@ -90,7 +90,9 @@
     rim_value, rim_state = shifted((value_pre[rim_start:], state_pre[rim_start:]), "seq", 1)
     value_act = depthwise(rim_value, value_pre, conv_value)
     state_act = depthwise(rim_state, state_pre, conv_state)
-    state_all = lax.all_gather(state_act, "tp", axis=1, tiled=True)
+    state_all = jnp.concatenate(
+        lax.all_to_all(jnp.stack([state_act] * lax.axis_size("tp")), "tp", 0, 0), axis=1
+    )
     heads_local = decay_log.shape[0]
     heads_total = heads_local * tp_count
     group_index = tp_index * heads_local // (heads_total // GROUPS)

time: 311 us -> 313 us (level)
  waiting for transfers between devices: 197 us -> 192 us
  starting transfers between devices: 5.58 us -> 9.78 us
  local copies, waits for them, and re-layouts: 7.12 us -> 10.6 us
    all_gather x1 -> x0, waiting for transfers between devices: 21 us -> none  [on_device(): state_all = lax.all_gather(state_act, 'tp', axis=1, tiled=True)]
    all_to_all x0 -> x1, waiting for transfers between devices: none -> 16.6 us  [on_device(): lax.all_to_all(jnp.stack([state_act] * lax.axis_size('tp')), 'tp', 0, 0)]
    all_to_all x0 -> x1, starting transfers between devices: none -> 4.24 us  [on_device(): lax.all_to_all(jnp.stack([state_act] * lax.axis_size('tp')), 'tp', 0, 0)]
where the time goes in v1:
time: 313 us; the launch traced here: 312 us
  waiting for transfers between devices  192 us (61%)
  matrix products  42.3 us (14%)
  blocking collectives  35.5 us (11%)
  between operations  13.4 us (4%)
  local copies, waits for them, and re-layouts  10.6 us (3%)
  starting transfers between devices  9.78 us (3%)
  other arithmetic  8.89 us (3%)
    psum x1, waiting for transfers between devices, on_device(): summed, total_squares = lax.psum((partial_value, local_squares), 'tp')  73.1 us
    reduce_scatter x1, waiting for transfers between devices, on_device(): lax.psum_scatter(contract_columns(out_down, normed), 'tp', scatter_dimens...  48.4 us
    all_gather x1, waiting for transfers between devices, on_device(): lax.all_gather(out_share, 'tp', axis=0, tiled=True)  29.3 us
    all_gather x1, waiting for transfers between devices, entering(): gathered = jax.tree.map(lambda a: lax.all_gather(a, axis), part)  23.7 us
    all_to_all x1, waiting for transfers between devices, on_device(): lax.all_to_all(jnp.stack([state_act] * lax.axis_size('tp')), 'tp', 0, 0)  16.6 us
    dot_general x1, matrix products, on_device(): within = jnp.einsum('hts,shp->thp', mixing, values, precision=highest)  14.3 us
    psum x1, blocking collectives, on_device(): summed, total_squares = lax.psum((partial_value, local_squares), 'tp')  13.9 us
    psum x1, blocking collectives, on_device(): lax.psum(jnp.sum(gated * gated, axis=1)[:, None] * selector[None, :], 'tp')  11.8 us
  transfers between devices with their start and end apart: 7, of which 6 were waited for; matrix products, arithmetic and copies ran while one was open for 3% of the time, Pallas kernels for 0%

profile of v1, /device:TPU:0, one launch (start us, length us, event | category | flops | bytes accessed | tf_op | source)
XLA Modules:
  0.0 312.3 jit_solution(3207882419836768127)
XLA Ops:
  6.5 0.0 all-reduce.2.cloned.1.call-start
  6.5 4.6 %fusion.29 = f32[512,1024]{1,0:T(8,128)} fusion(bf16[1024,1024]{1,0:T(8,128)(2,1)} %param.19, bf16[512,1024]{1,0:T(8,128)(2,1)} %param.17, f32[1024]{0:T(1024)} %param.18), kind=kOutput, calls=%fused_computation.51 | convolution fusion | flops 1075314688 | bytes 5246976 | tf_op jit(solution)/shard_map/dot_general | solution.py:78
  11.2 0.0 all-reduce.2.cloned.1.call-update
  11.2 1.2 copy-done.6
  12.4 0.3 fusion.20
  12.7 13.9 %psum.22 = f32[512]{0:T(512)S(1)} all-reduce(f32[512]{0:T(512)S(1)} %fusion.20), channel_id=1, replica_groups=mesh['seq'=8,'tp'=4] {'tp'}, use_global_device_ids=true, to_apply=%region_2.0 | all-reduce | flops 512 | bytes 4096 | tf_op jit(solution)/shard_map/psum | solution.py:79
  26.5 0.0 copy-done.15
  26.6 0.6 fusion.57
  27.2 73.1 %all-reduce.2.cloned.1.call-done = f32[512,1024]{1,0:T(8,128)} async-done(((f32[512,1024]{1,0:T(8,128)}), f32[512,1024]{1,0:T(8,128)}) %all-reduce.2.cloned.1.call-update) | async-done | bytes 2097168 | tf_op jit(solution)/shard_map/psum | solution.py:79
  100.3 1.8 multiply_convert_fusion.2
  102.1 0.0 copy-done.9
  102.2 0.0 copy-done.12
  102.2 0.0 copy-start.3
  102.2 0.4 fusion.28
  102.6 0.1 compare_select_fusion.1
  102.7 0.4 convolution_convert_fusion.2
  103.1 0.6 slice.90
  103.7 2.0 collective-permute-start.1
  105.7 1.1 reduce-window.6
  106.8 0.2 slice_reduce_fusion
  107.0 0.0 collective-permute-done.1
  107.0 0.7 maximum_convert_fusion.1
  107.8 1.0 multiply_convert_fusion.4
  108.8 1.1 stack.2
  109.9 4.2 %all-to-all-start = ((bf16[4,512,256]{2,1,0:T(8,128)(2,1)}), bf16[4,512,256]{2,1,0:T(8,128)(2,1)}, u32[]{:S(2)}, u32[]{:S(2)}) async-start(bf16[4,512,256]{2,1,0:T(8,128)(2,1)} %stack.2), calls=%async_computation | async-start | bytes 2097152 | tf_op jit(solution)/shard_map/all_to_all | solution.py:94
  114.1 0.0 all-gather.7.cloned.1.call-start
  114.2 2.8 convolution_convert_fusion.1
  117.0 3.4 %collective-permute-start = (bf16[3,1024]{1,0:T(4,128)(2,1)S(1)}, bf16[3,1024]{1,0:T(4,128)(2,1)S(1)}, u32[]{:S(2)}, u32[]{:S(2)}) collective-permute-start(bf16[3,1024]{1,0:T(4,128)(2,1)S(1)} %slice.85), channel_id=1, source_target_pairs={{0,4},{4,8},{8,12},{12,16},{16,20},{20,24},{24,28},{1,5},{5,9},{9,... | collective-permute-start | bytes 18440 | tf_op jit(solution)/shard_map/ppermute | solution.py:16
  120.5 0.1 copy_bitcast_fusion
  120.6 0.2 slice_reduce_fusion.1
  120.8 0.1 bitcast_exponential_fusion
  120.8 0.4 collective-permute-done
  121.3 0.3 maximum_convert_fusion
  121.6 1.3 multiply_convert_fusion.1
  122.9 1.3 copy.30
  124.2 16.6 %all-to-all-done = bf16[4,512,256]{2,1,0:T(8,128)(2,1)} async-done(((bf16[4,512,256]{2,1,0:T(8,128)(2,1)}), bf16[4,512,256]{2,1,0:T(8,128)(2,1)}, u32[]{:S(2)}, u32[]{:S(2)}) %all-to-all-start) | async-done | bytes 1048608 | tf_op jit(solution)/shard_map/all_to_all | solution.py:94
  140.8 1.4 copy.36
  142.1 1.0 copy-done.5
  143.1 2.0 fusion.13
  145.1 0.0 all-gather.7.cloned.1.call-update
  145.1 0.0 reduce-scatter.2.cloned.1.call-start
  145.2 0.1 iota_compare_fusion
  145.3 9.9 %all-gather.1 = f32[8,1,16]{2,1,0:T(1,128)S(1)} all-gather(f32[1,1,16]{2,1,0:T(1,128)S(1)} %bitcast.106), channel_id=1, replica_groups=mesh['seq'=8,'tp'=4] {'seq'}, dimensions={0}, use_global_device_ids=true | all-gather | bytes 576 | tf_op jit(solution)/shard_map/all_gather | solution.py:21
  155.2 2.3 fusion.42
  157.4 23.7 %all-gather.7.cloned.1.call-done = f32[128,64,128]{2,1,0:T(8,128)} async-done(((f32[16,64,128]{2,1,0:T(8,128)}), f32[128,64,128]{2,1,0:T(8,128)}) %all-gather.7.cloned.1.call-update) | async-done | bytes 4194320 | tf_op jit(solution)/shard_map/all_gather | solution.py:21
  181.2 0.2 while.12
  181.4 0.0 copy-start.2
  181.4 0.0 copy-start.16
  181.4 2.0 fusion.39
  183.5 0.0 copy-done.2
  183.5 14.3 %fusion.14 = f32[512,16,64]{0,2,1:T(8,128)} fusion(bf16[512,16,64]{0,2,1:T(8,128)(2,1)S(1)} %bitcast.90, f32[512,16,64]{0,2,1:T(8,128)S(1)} %fusion.39, f32[16,512]{1,0:T(8,128)S(1)} %get-tuple-element.66, f32[16,512]{1,0:T(8,128)S(1)} %get-tuple-element.64, f32[512,512]{1,0:T(8,128)S(1)} %copy-done.8, pred[512,512]{1,0:T(8,128)(4,1)S(1)} %iota_compare_fusion, ...), kind=kOutput, calls=%fused_computation.23 | convolution fusion | flops 3244818432 | bytes 6651968 | tf_op jit(solution)/shard_map/hts,shp->thp/dot_general | solution.py:114
  197.8 3.0 copy.34
  200.8 4.5 %multiply_reduce_fusion = (f32[512]{0:T(512)S(1)}, f32[512,1024]{1,0:T(8,128)}) fusion(f32[512,1024]{1,0:T(8,128)} %copy.34, bf16[512,1024]{1,0:T(8,128)(2,1)S(1)} %copy-done.4, bf16[1024,1024]{1,0:T(8,128)(2,1)S(1)} %copy-done), kind=kOutput, calls=%fused_computation.40 | convolution fusion | flops 1078459904 | bytes 7342080 | tf_op jit(solution)/shard_map/dot_general | solution.py:83
  205.3 0.1 broadcast_multiply_fusion
  205.4 11.8 %psum.23 = f32[512,4]{0,1:T(4,128)S(1)} all-reduce(f32[512,4]{0,1:T(4,128)S(1)} %broadcast_multiply_fusion), channel_id=1, replica_groups=mesh['seq'=8,'tp'=4] {'tp'}, use_global_device_ids=true, to_apply=%region_8.9 | all-reduce | flops 2048 | bytes 16384 | tf_op jit(solution)/shard_map/psum | solution.py:138
  217.2 0.1 multiply_reduce_fusion.1
  217.3 4.8 %convolution_bitcast_fusion = f32[1024,512]{0,1:T(8,128)} fusion(bf16[1024,1024]{1,0:T(8,128)(2,1)} %param.30, f32[512,1024]{1,0:T(8,128)} %get-tuple-element.77, f32[1024]{0:T(1024)S(1)} %copy-done.14, f32[512]{0:T(512)S(1)} %add_rsqrt_fusion), kind=kOutput, calls=%fused_computation.43 | convolution fusion | flops 1075314688 | bytes 6297600 | tf_op jit(solution)/shard_map/dot_general | solution.py:39
  222.2 0.0 reduce-scatter.2.cloned.1.call-update
  222.2 0.0 all-gather.5.cloned.1.call-start
  222.2 48.4 %reduce-scatter.2.cloned.1.call-done = f32[256,512]{0,1:T(8,128)} async-done(((f32[1024,512]{0,1:T(8,128)}), f32[256,512]{0,1:T(8,128)}) %reduce-scatter.2.cloned.1.call-update) | async-done | bytes 524304 | tf_op jit(solution)/shard_map/reduce_scatter | solution.py:143
  270.6 1.8 convert_element_type.79
  272.4 0.0 all-gather.5.cloned.1.call-update
  272.4 29.3 %all-gather.5.cloned.1.call-done = bf16[1024,512]{0,1:T(8,128)(2,1)} async-done(((bf16[256,512]{0,1:T(8,128)(2,1)}), bf16[1024,512]{0,1:T(8,128)(2,1)}) %all-gather.5.cloned.1.call-update) | async-done | bytes 1048592 | tf_op jit(solution)/shard_map/all_gather | solution.py:146
  301.7 4.1 %fusion.21 = bf16[512,1024]{1,0:T(8,128)(2,1)} fusion(bf16[512,1024]{1,0:T(8,128)(2,1)S(1)} %copy-done.7, bf16[1024,512]{0,1:T(8,128)(2,1)} %all-gather.5.cloned.1.call-done, bf16[1024,1024]{1,0:T(8,128)(2,1)} %param.31), kind=kOutput, calls=%fused_computation.30 | convolution fusion | flops 1075314688 | bytes 5242880 | tf_op jit(solution)/shard_map/dot_general | solution.py:33
  (35 shorter events, 0.2 us)
Async XLA Ops:
  6.5 194.3 %copy-start = (bf16[1024,1024]{1,0:T(8,128)(2,1)S(1)}, bf16[1024,1024]{1,0:T(8,128)(2,1)}, u32[]{:S(2)}) copy-start(bf16[1024,1024]{1,0:T(8,128)(2,1)} %param.20) | copy-start | bytes 6291460
  6.5 93.8 %all-reduce.2.cloned.1.call-start = ((), (), s32[]{:S(2)}) async-start(), calls=%async_computation.2 | async-start | bytes 4194304 | tf_op jit(solution)/shard_map/psum | solution.py:79
  11.2 1.2 copy-start.6
  11.2 15.4 %copy-start.15 = (f32[16]{0:T(128)S(1)}, f32[16]{0:T(128)}, u32[]{:S(2)}) copy-start(f32[16]{0:T(128)} %param.27) | copy-start | bytes 196
  11.2 15.4 %copy-start.11 = (f32[4,256]{1,0:T(4,128)S(1)}, f32[4,256]{1,0:T(4,128)}, u32[]{:S(2)}) copy-start(f32[4,256]{1,0:T(4,128)} %param.25) | copy-start | bytes 12292
  11.2 16.0 %copy-start.10 = (f32[4,1024]{1,0:T(4,128)S(1)}, f32[4,1024]{1,0:T(4,128)}, u32[]{:S(2)}) copy-start(f32[4,1024]{1,0:T(4,128)} %param.24) | copy-start | bytes 49156
  12.4 89.8 %copy-start.9 = (bf16[1024,16]{0,1:T(8,128)(2,1)S(1)}, bf16[1024,16]{0,1:T(8,128)(2,1)}, u32[]{:S(2)}) copy-start(bf16[1024,16]{0,1:T(8,128)(2,1)} %param.23) | copy-start | bytes 98308
  12.4 89.8 %copy-start.12 = (f32[16]{0:T(128)S(1)}, f32[16]{0:T(128)}, u32[]{:S(2)}) copy-start(f32[16]{0:T(128)} %param.26) | copy-start | bytes 196
  100.3 2.3 copy-start.13
  102.2 12.0 %copy-start.3 = (bf16[512,1024]{1,0:T(8,128)(2,1)}, bf16[512,1024]{1,0:T(8,128)(2,1)S(1)}, u32[]{:S(2)}) copy-start(bf16[512,1024]{1,0:T(8,128)(2,1)S(1)} %multiply_convert_fusion.2) | copy-start | bytes 3145732
  103.7 3.3 %collective-permute-start.1 = (bf16[3,256]{1,0:T(4,128)(2,1)}, bf16[3,256]{1,0:T(4,128)(2,1)}, u32[]{:S(2)}, u32[]{:S(2)}) collective-permute-start(bf16[3,256]{1,0:T(4,128)(2,1)} %slice.90), channel_id=1, source_target_pairs={{0,4},{4,8},{8,12},{12,16},{16,20},{20,24},{24,28},{1,5},{5,9},{9,... | collective-permute-start | bytes 4616 | tf_op jit(solution)/shard_map/ppermute | solution.py:16
  109.9 30.9 %all-to-all-start = ((bf16[4,512,256]{2,1,0:T(8,128)(2,1)}), bf16[4,512,256]{2,1,0:T(8,128)(2,1)}, u32[]{:S(2)}, u32[]{:S(2)}) async-start(bf16[4,512,256]{2,1,0:T(8,128)(2,1)} %stack.2), calls=%async_computation | async-start | bytes 2097152 | tf_op jit(solution)/shard_map/all_to_all | solution.py:94
  114.1 67.0 %all-gather.7.cloned.1.call-start = ((), (), s32[]{:S(2)}) async-start(), calls=%async_computation.5 | async-start | bytes 4718592 | tf_op jit(solution)/shard_map/all_gather | solution.py:21
  117.0 4.2 %collective-permute-start = (bf16[3,1024]{1,0:T(4,128)(2,1)S(1)}, bf16[3,1024]{1,0:T(4,128)(2,1)S(1)}, u32[]{:S(2)}, u32[]{:S(2)}) collective-permute-start(bf16[3,1024]{1,0:T(4,128)(2,1)S(1)} %slice.85), channel_id=1, source_target_pairs={{0,4},{4,8},{8,12},{12,16},{16,20},{20,24},{24,28},{1,5},{5,9},{9,... | collective-permute-start | bytes 18440 | tf_op jit(solution)/shard_map/ppermute | solution.py:16
  124.2 18.9 %copy-start.1 = (bf16[512,1024]{0,1:T(8,128)(2,1)S(1)}, bf16[512,1024]{0,1:T(8,128)(2,1)}, u32[]{:S(2)}) copy-start(bf16[512,1024]{0,1:T(8,128)(2,1)} %copy.30) | copy-start | bytes 3145732
  142.1 1.0 copy-start.5
  145.1 125.5 %reduce-scatter.2.cloned.1.call-start = ((), (), s32[]{:S(2)}) async-start(), calls=%async_computation.3 | async-start | bytes 2621440 | tf_op jit(solution)/shard_map/reduce_scatter | solution.py:143
  181.4 2.1 copy-start.2
  181.4 2.1 copy-start.8
  181.4 2.1 copy-start.16
  197.8 3.0 copy-start.4
  200.8 16.5 %copy-start.14 = (f32[1024]{0:T(1024)S(1)}, f32[1024]{0:T(1024)}, u32[]{:S(2)}) copy-start(f32[1024]{0:T(1024)} %param.29) | copy-start | bytes 12292
  222.2 79.5 %copy-start.7 = (bf16[512,1024]{1,0:T(8,128)(2,1)S(1)}, bf16[512,1024]{1,0:T(8,128)(2,1)}, u32[]{:S(2)}) copy-start(bf16[512,1024]{1,0:T(8,128)(2,1)} %param.17) | copy-start | bytes 3145732
  222.2 79.5 %all-gather.5.cloned.1.call-start = ((), (), s32[]{:S(2)}) async-start(), calls=%async_computation.4 | async-start | bytes 1310720 | tf_op jit(solution)/shard_map/all_gather | solution.py:146
Sparse Core Ops, SparseCore 0:
  11.3 88.9 all-reduce.1
  145.2 35.8 all-gather.6
  222.3 48.2 reduce-scatter.1
  272.5 29.1 all-gather.4
